TPU v7x, 32 devices: a whole 2x2x4 slice. The times are simulated.
32 devices in a mesh: pair: 4 (over y, x), grow: 4 (over z), gcol: 2 (over core).
Axes of the slice: x: 2, y: 2, z: 4, core: 2. Of those that a mesh axis runs over, the one named last changes fastest.
Arguments:
- valence: bfloat16 [16, 96, 9216], P(None, 'grow'), may hold values from -6 to 6
- conduction: bfloat16 [16, 96, 9216], P(('pair', 'gcol'), 'grow'), may hold values from -6 to 6
- val_energy: float32 [16], replicated, may hold values from -10 to -1
- cond_energy: float32 [16], replicated, may hold values from 1 to 20
- val_occupation: int32 [16], replicated, may hold values from 1 to 16
- gvectors: int32 [3, 3840], replicated, may hold values from -12 to 12, as said below
Outputs:
- chi_zero: float32 [7680, 7680], P(('pair', 'gcol'), 'grow')
Inputs may be any that keep to these rules, and one draw needn't show every extreme that they name: gvectors holds 3840 distinct wave vectors; the first component lies in 1 .. 12, the other two in -12 .. 12.
All inputs are finite; a program needn't handle non-finite values.
Results may differ from a plain program's by a relative error of at most 0.02.
Values may be sent and summed in bfloat16 or wider, within the bound.
A program may use at most 128 MiB of HBM per device.

v0:
```python
import math

import jax
import jax.numpy as jnp
from jax import lax
from jax.sharding import PartitionSpec as P

N = 96
RAD = 12
KG = 3840
NV = 16


def wave_tables(positions, frequencies):
    phases = jnp.mod(positions[:, None] * frequencies[None, :], N).astype(jnp.float32) * (
        2.0 * math.pi / N
    )
    return (jnp.cos(phases), jnp.sin(phases))


def build_tables(x_positions):
    all_freq = jnp.arange(-RAD, RAD + 1, dtype=jnp.int32)
    pos_freq = jnp.arange(1, RAD + 1, dtype=jnp.int32)
    positions = jnp.arange(N, dtype=jnp.int32)
    cosine, sine_part = wave_tables(positions, all_freq)
    z_table = jnp.concatenate([cosine, sine_part], 1).astype(jnp.bfloat16)
    y_table = jnp.stack(
        [jnp.stack([cosine, sine_part], 1), jnp.stack([-sine_part, cosine], 1)], 1
    ).astype(jnp.bfloat16)
    x_cos, x_sin = wave_tables(x_positions, pos_freq)
    x_table = jnp.stack([jnp.stack([x_cos, -x_sin], 1), jnp.stack([-x_sin, -x_cos], 1)], 1).astype(
        jnp.bfloat16
    )
    return (z_table, y_table, x_table)


def pair_product(left_rows, right_rows):
    return lax.dot_general(
        left_rows, right_rows, (((0,), (0,)), ((), ())), preferred_element_type=jnp.float32
    )


def body(valence, conduction, val_energy, cond_energy, val_occupation, gvectors):
    pair_count = lax.axis_size("pair")
    gcol_count = lax.axis_size("gcol")
    planes = valence.shape[1]
    cond_bands = conduction.shape[0]
    extent = 2 * RAD + 1
    local_pairs = cond_bands * NV
    x_positions = lax.axis_index("grow") * planes + jnp.arange(planes, dtype=jnp.int32)
    z_table, y_table, x_table = build_tables(x_positions)
    flat_index = ((gvectors[0] - 1) * extent + gvectors[1] + RAD) * extent + gvectors[2] + RAD
    density = conduction[:, None] * valence[None]
    section_one = jnp.dot(
        density.reshape(-1, N), z_table, preferred_element_type=jnp.float32
    ).astype(jnp.bfloat16)
    section_one = section_one.reshape(local_pairs * planes, N, 2, extent)
    second = jnp.einsum(
        "ayik,yioj->aojk", section_one, y_table, preferred_element_type=jnp.float32
    ).astype(jnp.bfloat16)
    second = second.reshape(local_pairs, planes, 2, extent * extent)
    section_three = jnp.einsum(
        "pxoq,xosm->psmq", second, x_table, preferred_element_type=jnp.float32
    )
    section_three = section_three.reshape(local_pairs, 2, RAD * extent * extent)
    picked = jnp.take(section_three, flat_index, axis=2).reshape(local_pairs, 2 * KG)
    summed = lax.psum_scatter(
        picked.astype(jnp.bfloat16), "grow", scatter_dimension=1, tiled=True
    ).astype(jnp.float32)
    first_band = (lax.axis_index("pair") * gcol_count + lax.axis_index("gcol")) * cond_bands
    own_energy = lax.dynamic_slice_in_dim(cond_energy, first_band, cond_bands, 0)
    weight = val_occupation.astype(jnp.float32)[None, :] / (
        4.0 * (own_energy[:, None] - val_energy[None, :])
    )
    factor = (jnp.sqrt(weight) * (1.0 / N**1.5)).reshape(local_pairs, 1)
    weighted = (summed * factor).astype(jnp.bfloat16)
    prefactor = -1.0 / math.sqrt(pair_count * gcol_count * local_pairs)
    full_rows = lax.all_gather(weighted, "grow", axis=1, tiled=True)
    row_part = lax.all_to_all(full_rows, "pair", split_axis=1, concat_axis=0, tiled=True)
    partial_value = pair_product(row_part, lax.all_gather(weighted, "pair", axis=0, tiled=True))
    return lax.psum_scatter(
        (partial_value * prefactor).astype(jnp.bfloat16), "gcol", scatter_dimension=0, tiled=True
    ).astype(jnp.float32)


def solution(mesh):
    return jax.shard_map(
        body,
        mesh=mesh,
        in_specs=(P(None, "grow", None), P(("pair", "gcol"), "grow", None), P(), P(), P(), P()),
        out_specs=P(("pair", "gcol"), "grow"),
        check_vma=False,
    )
```

profile of v0, /device:TPU:27, one launch (start us, length us, event | category | flops | bytes accessed | tf_op | source)
XLA Modules:
  0.0 242.2 jit_solution(5478735523802788181)
XLA Ops:
  6.5 0.0 reduce-scatter.7.cloned.1.call-start
  6.5 0.2 cosine_convert_fusion
  6.7 0.2 fusion.25
  6.9 9.0 %broadcast_multiply_fusion = bf16[2,16,24,9216]{3,2,1,0:T(8,128)(2,1)} fusion(bf16[16,24,9216]{2,1,0:T(8,128)(2,1)} %param.6, bf16[2,24,9216]{2,1,0:T(8,128)(2,1)} %param.7), kind=kLoop, calls=%fused_computation.5 | loop fusion | flops 7077888 | bytes 22118400 | tf_op jit(solution)/shard_map/mul | solution.py:53
  15.8 27.3 %mul.245 = bf16[73728,96]{1,0:T(8,128)(2,1)} reshape(bf16[2,16,24,9216]{3,2,1,0:T(8,128)(2,1)} %broadcast_multiply_fusion) | data formatting | bytes 28311552 | tf_op jit(solution)/shard_map/mul | solution.py:53
  43.1 16.8 %convolution_convert_fusion = bf16[73728,50]{0,1:T(8,128)(2,1)} fusion(bf16[73728,96]{1,0:T(8,128)(2,1)} %mul.245, bf16[96,25]{0,1:T(8,128)(2,1)S(1)} %get-tuple-element.19, bf16[96,25]{0,1:T(8,128)(2,1)S(1)} %get-tuple-element.18), kind=kOutput, calls=%fused_computation.1 | convolution fusion | flops 711494400 | bytes 21538176 | tf_op jit(solution)/shard_map/dot_general | solution.py:54
  60.0 12.8 %reshape.389 = bf16[768,96,2,25]{1,0,3,2:T(8,128)(2,1)} reshape(bf16[73728,50]{0,1:T(8,128)(2,1)} %convolution_convert_fusion) | data formatting | bytes 14745600 | tf_op jit(solution)/shard_map/reshape | solution.py:57
  72.7 6.8 %fusion.2 = bf16[768,2,25,25]{0,2,3,1:T(8,128)(2,1)S(1)} fusion(bf16[768,96,2,25]{1,0,3,2:T(8,128)(2,1)} %reshape.389, bf16[96,1,2,25]{0,3,1,2:T(8,128)(2,1)S(1)} %get-tuple-element.9, bf16[96,1,2,25]{0,3,1,2:T(8,128)(2,1)S(1)} %get-tuple-element.8), kind=kOutput, calls=%fused_computation.7 | convolution fusion | flops 369638400 | bytes 9312000 | tf_op jit(solution)/shard_map/ayik,yioj->aojk/dot_general | solution.py:58
  79.6 2.0 copy.44
  81.6 18.9 %reshape.390 = bf16[32,24,2,625]{1,0,2,3:T(8,128)(2,1)} reshape(bf16[768,2,25,25]{0,1,3,2:T(2,128)(2,1)S(1)} %copy.44) | data formatting | bytes 3840000 | tf_op jit(solution)/shard_map/reshape | solution.py:61
  100.5 0.0 copy-start
  100.5 9.2 %copy.45 = bf16[32,24,2,625]{3,1,2,0:T(8,128)(2,1)S(1)} copy(bf16[32,24,2,625]{1,0,2,3:T(8,128)(2,1)} %reshape.390) | data formatting | bytes 3840000 | tf_op jit(solution)/shard_map/reshape | solution.py:61
  109.7 0.1 fusion.37
  109.9 0.5 fusion.7
  110.4 0.0 copy-start.2
  110.4 0.0 copy-start.3
  110.4 0.0 copy-start.1
  110.5 5.6 %copy.56 = bf16[32,2,12,625]{0,1,3,2:T(2,128)(2,1)} copy(bf16[32,2,12,625]{3,2,0,1:T(8,128)(2,1)S(1)} %fusion.7) | data formatting | bytes 1920000 | tf_op jit(solution)/shard_map/reshape | solution.py:65
  116.1 0.0 copy-done
  116.1 0.1 add_reduce_fusion.1
  116.2 0.1 fusion.28
  116.3 12.3 %gather_fusion = bf16[3840,32,2]{1,2,0:T(2,128)(2,1)S(1)} fusion(bf16[32,2,7500]{0,1,2:T(2,128)(2,1)} %bitcast.75, s32[4096]{0:T(1024)S(1)} %pad_clamp_fusion), kind=kCustom, calls=%fused_computation | custom fusion | bytes 998400 | tf_op jit(solution)/shard_map/jit(_take)/gather | solution.py:66
  128.6 2.0 copy.47
  130.6 0.1 copy.60
  130.7 0.1 select_convert_fusion
  130.8 1.7 copy.57
  132.5 0.0 reduce-scatter.7.cloned.1.call-update
  132.5 0.0 copy-done.2
  132.6 0.0 copy-done.3
  132.6 0.1 dynamic_slice.3
  132.6 0.0 copy-done.1
  132.7 0.1 sqrt_multiply_fusion
  132.7 0.1 reshape.397
  132.8 40.5 %reduce-scatter.7.cloned.1.call-done = bf16[1920,32]{1,0:T(8,128)(2,1)} async-done(((bf16[7680,32]{1,0:T(8,128)(2,1)}), bf16[1920,32]{1,0:T(8,128)(2,1)}) %reduce-scatter.7.cloned.1.call-update) | async-done | bytes 122896
  173.3 1.2 copy.58
  174.5 0.1 multiply_convert_fusion.1
  174.6 12.8 %all_gather.6 = bf16[32,7680]{1,0:T(8,128)(2,1)S(1)} all-gather(bf16[32,1920]{1,0:T(8,128)(2,1)S(1)} %multiply_convert_fusion.1), channel_id=1, replica_groups=mesh['pair'=4,'grow'=4,'gcol'=2] {'grow'}, dimensions={1}, use_global_device_ids=true | all-gather | bytes 614400 | tf_op jit(solution)/shard_map/all_gather | solution.py:78
  187.4 0.8 copy.62
  188.2 3.9 %all-to-all-start = ((bf16[32,4,1920]{2,0,1:T(8,128)(2,1)}), bf16[32,4,1920]{2,0,1:T(8,128)(2,1)S(1)}, u32[]{:S(2)}, u32[]{:S(2)}) async-start(bf16[32,4,1920]{2,0,1:T(8,128)(2,1)} %bitcast.73), calls=%async_computation | async-start | bytes 983040 | tf_op jit(solution)/shard_map/all_to_all | solution.py:79
  192.1 0.0 reduce-scatter.5.cloned.1.call-start
  192.1 11.1 %all_gather.7 = bf16[128,1920]{1,0:T(8,128)(2,1)S(1)} all-gather(bf16[32,1920]{1,0:T(8,128)(2,1)S(1)} %multiply_convert_fusion.1), channel_id=1, replica_groups=mesh['pair'=4,'grow'=4,'gcol'=2] {'pair'}, dimensions={0}, use_global_device_ids=true | all-gather | bytes 614400 | tf_op jit(solution)/shard_map/all_gather | solution.py:80
  203.2 0.0 all-to-all-done
  203.2 5.2 %multiply_convert_fusion = bf16[1920,1920]{1,0:T(8,128)(2,1)} fusion(bf16[128,1920]{1,0:T(8,128)(2,1)S(1)} %bitcast.77, bf16[128,1920]{1,0:T(8,128)(2,1)S(1)} %all_gather.7), kind=kOutput, calls=%fused_computation.2 | convolution fusion | flops 951091200 | bytes 8355840 | tf_op jit(solution)/shard_map/dot_general | solution.py:38
  208.4 0.0 reduce-scatter.5.cloned.1.call-update
  208.4 21.4 %reduce-scatter.5.cloned.1.call-done = bf16[960,1920]{1,0:T(8,128)(2,1)} async-done(((bf16[1920,1920]{1,0:T(8,128)(2,1)}), bf16[960,1920]{1,0:T(8,128)(2,1)}) %reduce-scatter.5.cloned.1.call-update) | async-done | bytes 3686416 | tf_op jit(solution)/shard_map/reduce_scatter | solution.py:81
  229.8 5.6 %convert_element_type.87 = f32[960,1920]{1,0:T(8,128)} convert(bf16[960,1920]{1,0:T(8,128)(2,1)} %reduce-scatter.5.cloned.1.call-done) | non-fusion elementwise | flops 1843200 | bytes 11059200 | tf_op jit(solution)/shard_map/convert_element_type | solution.py:83
  (10 shorter events, 0.1 us)
Async XLA Ops:
  6.5 166.7 %reduce-scatter.7.cloned.1.call-start = ((), (), s32[]{:S(2)}) async-start(), calls=%async_computation.4 | async-start | bytes 2457600
  100.5 15.6 %copy-start = (s32[3,3840]{1,0:T(4,128)S(1)}, s32[3,3840]{1,0:T(4,128)}, u32[]{:S(2)}) copy-start(s32[3,3840]{1,0:T(4,128)} %param.11) | copy-start | bytes 138244
  110.4 22.1 %copy-start.2 = (s32[16]{0:T(128)S(1)}, s32[16]{0:T(128)}, u32[]{:S(2)}) copy-start(s32[16]{0:T(128)} %param.10) | copy-start | bytes 196
  110.4 22.1 %copy-start.3 = (f32[16]{0:T(128)S(1)}, f32[16]{0:T(128)}, u32[]{:S(2)}) copy-start(f32[16]{0:T(128)} %param.9) | copy-start | bytes 196
  110.4 22.2 %copy-start.1 = (f32[16]{0:T(128)S(1)}, f32[16]{0:T(128)}, u32[]{:S(2)}) copy-start(f32[16]{0:T(128)} %param.8) | copy-start | bytes 196
  188.2 15.0 %all-to-all-start = ((bf16[32,4,1920]{2,0,1:T(8,128)(2,1)}), bf16[32,4,1920]{2,0,1:T(8,128)(2,1)S(1)}, u32[]{:S(2)}, u32[]{:S(2)}) async-start(bf16[32,4,1920]{2,0,1:T(8,128)(2,1)} %bitcast.73), calls=%async_computation | async-start | bytes 983040 | tf_op jit(solution)/shard_map/all_to_all | solution.py:79
  192.1 37.7 %reduce-scatter.5.cloned.1.call-start = ((), (), s32[]{:S(2)}) async-start(), calls=%async_computation.3 | async-start | bytes 11059200 | tf_op jit(solution)/shard_map/reduce_scatter | solution.py:81
Sparse Core Ops, SparseCore 0:
  132.7 40.5 reduce-scatter.6
  208.5 21.1 reduce-scatter.4
where the time goes:
time: 245 us; the launch traced here: 242 us
  local copies, waits for them, and re-layouts  94.1 us (38%)
  waiting for transfers between devices  61.9 us (25%)
  matrix products  29.4 us (12%)
  blocking collectives  23.9 us (10%)
  other arithmetic  15.5 us (6%)
  between operations  13.6 us (6%)
  starting transfers between devices  3.91 us (2%)
    unnamed x3, waiting for transfers between devices  40.5 us
    reshape x2, local copies, waits for them, and re-layouts, body(): second = second.reshape(local_pairs, planes, 2, extent * extent)  28.1 us
    mul x1, local copies, waits for them, and re-layouts, body(): density = conduction[:, None] * valence[None]  27.3 us
    reduce_scatter x1, waiting for transfers between devices, body(): lax.psum_scatter((partial_value * prefactor).astype(jnp.bfloat16), 'gcol'...  21.4 us
    dot_general x1, matrix products, body(): jnp.dot(density.reshape(-1, N), z_table, preferred_element_type=jnp.float32)  16.8 us
    gather x2, local copies, waits for them, and re-layouts, body(): jnp.take(section_three, flat_index, axis=2).reshape(local_pairs, 2 * KG)  14.2 us
    all_gather x1, blocking collectives, body(): full_rows = lax.all_gather(weighted, 'grow', axis=1, tiled=True)  12.8 us
    reshape x1, local copies, waits for them, and re-layouts, body(): section_one = section_one.reshape(local_pairs * planes, N, 2, extent)  12.8 us
  transfers between devices with their start and end apart: 3, of which 2 were waited for; matrix products, arithmetic and copies ran while one was open for 0% of the time, Pallas kernels for 0%

commit v1 on v0

--- a/solution.py
+++ b/solution.py
@@ -1,8 +1,13 @@
 import math
+
+import functools
 
 import jax
 import jax.numpy as jnp
+import numpy as np
 from jax import lax
+from jax.experimental import pallas as pl
+from jax.experimental.pallas import tpu as pltpu
 from jax.sharding import PartitionSpec as P
 
 N = 96
@@ -83,9 +88,325 @@
     ).astype(jnp.float32)
 
 
+EXT = 2 * RAD + 1
+QUARTER = N * N // 4
+STEP = 8 * N
+CLASSES = ((0, 4, 8, 12), (2, 6, 10), (1, 3, 5, 7, 9, 11))
+WIDTHS = (128, 128, 256)
+ROWS = (104, 80, 152)
+STARTS = (0, 104, 184)
+NR = 336
+
+
+def half_plane_tables():
+    total = 2 * sum(WIDTHS)
+    left = np.zeros((2, N // 4, total), np.float32)
+    right = np.zeros((2, N, total), np.float32)
+    sign = np.zeros((1, WIDTHS[2]), np.float32)
+    y = np.arange(N // 4)[:, None]
+    z = np.arange(N)[:, None]
+    k = np.arange(-RAD, RAD + 1)
+    base = 0
+    for freqs, width in zip(CLASSES, WIDTHS):
+        jj = np.repeat(np.array(freqs), EXT)[None]
+        kk = np.tile(k, len(freqs))[None]
+        count = jj.shape[1]
+        ay = 2 * np.pi * ((jj * y) % N) / N
+        az = 2 * np.pi * ((kk * z) % N) / N
+        for part in range(2):
+            cols = slice(base + part * width, base + part * width + count)
+            left[0, :, cols] = np.sin(ay) if part else np.cos(ay)
+            left[1, :, cols] = np.cos(ay) if part else -np.sin(ay)
+            right[0, :, cols] = np.cos(az)
+            right[1, :, cols] = np.sin(az)
+        base += 2 * width
+    jj = np.repeat(np.array(CLASSES[2]), EXT)
+    sign[0, : jj.size] = np.where(jj % 4 == 1, 1.0, -1.0)
+    return left, right, sign
+
+
+def plane_table(pairs):
+    x = np.arange(N)[:, None]
+    a = np.arange(1, RAD + 1)[None]
+    ang = 2 * np.pi * ((a * x) % N) / N
+    c, s = np.cos(ang), np.sin(ang)
+    tab = np.stack([np.stack([c, -s, c, -s], -1), np.stack([-s, -c, s, c], -1)])
+    return np.repeat(tab.reshape(2, N, RAD * 4), pairs, axis=2).astype(np.float32)
+
+
+def transform_kernel(
+    idx, grow, v0, v1, v2, v3, c0, c1, c2, c3, left, right, sign, xtab, factor, out,
+    ee, eo, oo, tab, acc_ee, acc_eo, acc_o, xmat, sec, got,
+):
+    step = pl.program_id(0)
+    nv, planes, _ = v0.shape
+    bands = c0.shape[0]
+    pairs = nv * bands
+    rows = pairs * planes
+    lanes = 4 * pairs
+    f32 = jnp.float32
+
+    @pl.when(step == 0)
+    def _():
+        acc_ee[...] = jnp.zeros_like(acc_ee)
+        acc_eo[...] = jnp.zeros_like(acc_eo)
+        acc_o[...] = jnp.zeros_like(acc_o)
+
+    for y in range(STEP // N):
+        yy = step * (STEP // N) + y
+        l1 = left[0, pl.ds(yy, 1), :]
+        l2 = left[1, pl.ds(yy, 1), :]
+        tab[y * N : (y + 1) * N, :] = (l1 * right[0] + l2 * right[1]).astype(jnp.bfloat16)
+
+    def products(v, carry):
+        vals = [ref[pl.ds(2 * v, 2)].astype(f32) for ref in (v0, v1, v2, v3)]
+        for c in range(bands):
+            d0, d1, d2, d3 = [
+                (val * ref[c].astype(f32)[None]).reshape(2 * planes, STEP)
+                for val, ref in zip(vals, (c0, c1, c2, c3))
+            ]
+            e0, e1 = d0 + d2, d1 + d3
+            at = pl.multiple_of(c * nv * planes + v * 2 * planes, 16)
+            where = pl.ds(at, 2 * planes)
+            ee[where, :] = (e0 + e1).astype(jnp.bfloat16)
+            eo[where, :] = (e0 - e1).astype(jnp.bfloat16)
+            oo[where, :] = (d0 - d2).astype(jnp.bfloat16)
+            oo[pl.ds(pl.multiple_of(rows + at, 16), 2 * planes), :] = (d1 - d3).astype(jnp.bfloat16)
+        return carry
+
+    lax.fori_loop(0, nv // 2, products, 0)
+
+    def multiply(i, carry):
+        block = rows // 2
+        part = pl.ds(pl.multiple_of(i * block, 16), block)
+        acc_ee[part, :] += jnp.dot(ee[part, :], tab[:, 0:256], preferred_element_type=f32)
+        acc_eo[part, :] += jnp.dot(eo[part, :], tab[:, 256:512], preferred_element_type=f32)
+        for h in range(2):
+            at = pl.ds(pl.multiple_of(h * rows + i * block, 16), block)
+            acc_o[at, :] += jnp.dot(oo[at, :], tab[:, 512:1024], preferred_element_type=f32)
+        return carry
+
+    lax.fori_loop(0, 2, multiply, 0)
+
+    @pl.when(step == pl.num_programs(0) - 1)
+    def _():
+        own = lax.broadcasted_iota(jnp.int32, (1, RAD * lanes), 1) % pairs
+
+        def place(p, carry):
+            for h in range(2):
+                two = []
+                for u in range(2):
+                    two.append(jnp.where(own == 2 * p + u, xtab[h], 0.0))
+                at = pl.multiple_of(h * rows + p * 2 * planes, 16)
+                xmat[pl.ds(at, 2 * planes), :] = jnp.concatenate(two, 0).astype(jnp.bfloat16)
+            return carry
+
+        lax.fori_loop(0, pairs // 2, place, 0)
+        w = WIDTHS[2]
+        top, low = acc_o[0:rows, :], acc_o[rows : 2 * rows, :]
+        odd_p = top[:, 0:w] - sign[...] * low[:, w:]
+        odd_q = top[:, w:] + sign[...] * low[:, 0:w]
+        groups = (
+            (acc_ee[:, 0:128], acc_ee[:, 128:256]),
+            (acc_eo[:, 0:128], acc_eo[:, 128:256]),
+            (odd_p, odd_q),
+        )
+        for (p_part, q_part), count, start in zip(groups, ROWS, STARTS):
+            p_rows = p_part.T[0:count].astype(jnp.bfloat16)
+            q_rows = q_part.T[0:count].astype(jnp.bfloat16)
+            summed = jnp.dot(p_rows, xmat[0:rows, :], preferred_element_type=f32)
+            summed += jnp.dot(q_rows, xmat[rows : 2 * rows, :], preferred_element_type=f32)
+            for a in range(RAD):
+                piece = summed[:, a * lanes : (a + 1) * lanes] * factor[...]
+                sec[a * NR + start : a * NR + start + count, :] = piece
+                at = (RAD + a) * NR + start
+                sec[at : at + count, :] = pltpu.roll(piece, lanes // 2, 1)
+
+        def pick(i, carry):
+            for u in range(16):
+                got[pl.ds(i * 16 + u, 1), :] = sec[pl.ds(idx[i * 16 + u], 1), :]
+            return carry
+
+        lax.fori_loop(0, KG // 16, pick, 0)
+        for i in range(KG // 384):
+            turned = got[i * 384 : (i + 1) * 384, :].T.astype(jnp.bfloat16)
+            out[:, i * 384 : (i + 1) * 384] = turned[0:pairs]
+            out[:, KG + i * 384 : KG + (i + 1) * 384] = turned[pairs : 2 * pairs]
+
+
+def pair_transform(valence, conduction, factor, gvectors):
+    nv, planes, _ = valence.shape
+    bands = conduction.shape[0]
+    pairs = nv * bands
+    rows = pairs * planes
+    lanes = 4 * pairs
+    steps = QUARTER // STEP
+    a, b, d = gvectors[0], gvectors[1], gvectors[2]
+    flip = b < 0
+    j = jnp.abs(b)
+    k = jnp.where(flip, -d, d) + RAD
+    row = jnp.where(
+        j % 2 == 1,
+        STARTS[2] + (j // 2) * EXT,
+        jnp.where(j % 4 == 2, STARTS[1], STARTS[0]) + (j // 4) * EXT,
+    )
+    index = (jnp.where(flip, RAD, 0) + a - 1) * NR + row + k
+    grow = lax.axis_index("grow").astype(jnp.int32).reshape(1)
+    left, right, sign = half_plane_tables()
+    whole = lambda shape: pl.BlockSpec(shape, lambda i, idx, g: (0,) * len(shape))
+    piece = lambda n, q: pl.BlockSpec(
+        (n, planes, STEP), lambda i, idx, g, q=q: (0, 0, q * steps + i)
+    )
+    call = pl.pallas_call(
+        transform_kernel,
+        out_shape=jax.ShapeDtypeStruct((pairs, 2 * KG), jnp.bfloat16),
+        grid_spec=pltpu.PrefetchScalarGridSpec(
+            num_scalar_prefetch=2,
+            grid=(steps,),
+            in_specs=[piece(nv, q) for q in range(4)]
+            + [piece(bands, q) for q in range(4)]
+            + [
+                whole(left.shape),
+                whole(right.shape),
+                whole(sign.shape),
+                pl.BlockSpec((2, planes, RAD * lanes), lambda i, idx, g: (0, g[0], 0)),
+                whole((1, lanes)),
+            ],
+            out_specs=whole((pairs, 2 * KG)),
+            scratch_shapes=[
+                pltpu.VMEM((rows, STEP), jnp.bfloat16),
+                pltpu.VMEM((rows, STEP), jnp.bfloat16),
+                pltpu.VMEM((2 * rows, STEP), jnp.bfloat16),
+                pltpu.VMEM((STEP, 2 * sum(WIDTHS)), jnp.bfloat16),
+                pltpu.VMEM((rows, 2 * WIDTHS[0]), jnp.float32),
+                pltpu.VMEM((rows, 2 * WIDTHS[1]), jnp.float32),
+                pltpu.VMEM((2 * rows, 2 * WIDTHS[2]), jnp.float32),
+                pltpu.VMEM((2 * rows, RAD * lanes), jnp.bfloat16),
+                pltpu.VMEM((2 * RAD * NR, lanes), jnp.float32),
+                pltpu.VMEM((KG, lanes), jnp.float32),
+            ],
+        ),
+        compiler_params=pltpu.CompilerParams(vmem_limit_bytes=60 * 1024 * 1024),
+    )
+    return call(
+        index, grow, *([valence] * 4), *([conduction] * 4), left, right, sign,
+        plane_table(pairs), jnp.tile(factor.reshape(1, pairs), (1, 4)),
+    )
+
+
+def exchange_kernel(
+    part, cols, rows, inbox, blocks, sends, recvs,
+):
+    count, _, width = blocks.shape
+    p, g, c = lax.axis_index("pair"), lax.axis_index("grow"), lax.axis_index("gcol")
+    me = p * 2 + c
+    f32 = jnp.float32
+    turn = lambda at, k: lax.rem(at + k, count)
+    barrier = pltpu.get_barrier_semaphore()
+    for k in range(1, count):
+        pl.semaphore_signal(barrier, inc=1, device_id=(p, turn(g, k), c))
+        pl.semaphore_signal(barrier, inc=1, device_id=(turn(p, k), g, c))
+    pl.semaphore_signal(barrier, inc=1, device_id=(p, g, 1 - c))
+    pl.semaphore_wait(barrier, 2 * count - 1)
+
+    def send(src, dst, sem, to):
+        copy = pltpu.make_async_remote_copy(
+            src_ref=src, dst_ref=dst, send_sem=sends.at[sem], recv_sem=recvs.at[sem],
+            device_id=to, device_id_type=pl.DeviceIdType.MESH,
+        )
+        copy.start()
+        return copy
+
+    block = lambda at: pl.ds(pl.multiple_of(at * width, 128), width)
+    first = [
+        send(part.at[:, block(turn(g, k))], inbox.at[k - 1], k - 1, (p, turn(g, k), c))
+        for k in range(1, count)
+    ]
+    total = part[:, block(g)].astype(f32)
+    for k in range(1, count):
+        first[k - 1].wait_recv()
+        total += inbox[k - 1].astype(f32)
+    mine = total.astype(jnp.bfloat16)
+    blocks[g] = mine
+    cols[me] = mine
+    n = count - 1
+    along = [
+        send(blocks.at[g], blocks.at[g], n + k - 1, (p, turn(g, k), c)) for k in range(1, count)
+    ]
+    flat = [
+        send(cols.at[me], cols.at[me], 2 * n + k - 1, (turn(p, k), g, c)) for k in range(1, count)
+    ]
+    over = [send(cols.at[me], cols.at[me], 4 * n, (p, g, 1 - c))]
+    for copy in along:
+        copy.wait_recv()
+    across = [
+        send(blocks.at[turn(p, k)], rows.at[me], 3 * n + k - 1, (turn(p, k), g, c))
+        for k in range(1, count)
+    ]
+    rows[me] = blocks[p]
+    over.append(send(rows.at[me], rows.at[me], 4 * n + 1, (p, g, 1 - c)))
+    for k in range(1, count):
+        slot = turn(p, count - k) * 2 + c
+        flat[k - 1].wait_recv()
+        over.append(send(cols.at[slot], cols.at[slot], 4 * n + 1 + k, (p, g, 1 - c)))
+    for k in range(1, count):
+        slot = turn(p, count - k) * 2 + c
+        across[k - 1].wait_recv()
+        over.append(send(rows.at[slot], rows.at[slot], 5 * n + 1 + k, (p, g, 1 - c)))
+    for copy in over:
+        copy.wait_recv()
+    for copy in first + along + flat + across + over:
+        copy.wait_send()
+
+
+def exchange(part, count):
+    pairs, total = part.shape
+    width = total // count
+    gathered = jax.ShapeDtypeStruct((2 * count, pairs, width), jnp.bfloat16)
+    vmem = pl.BlockSpec(memory_space=pltpu.VMEM)
+    sems = 6 * (count - 1) + 2
+    return pl.pallas_call(
+        exchange_kernel,
+        out_shape=(gathered, gathered),
+        in_specs=[vmem],
+        out_specs=(vmem, vmem),
+        scratch_shapes=[
+            pltpu.VMEM((count - 1, pairs, width), jnp.bfloat16),
+            pltpu.VMEM((count, pairs, width), jnp.bfloat16),
+            pltpu.SemaphoreType.DMA((sems,)),
+            pltpu.SemaphoreType.DMA((sems,)),
+        ],
+        compiler_params=pltpu.CompilerParams(collective_id=0, has_side_effects=True),
+    )(part)
+
+
+def fast_body(valence, conduction, val_energy, cond_energy, val_occupation, gvectors):
+    pair_count = lax.axis_size("pair")
+    gcol_count = lax.axis_size("gcol")
+    cond_bands = conduction.shape[0]
+    local_pairs = cond_bands * valence.shape[0]
+    first_band = (lax.axis_index("pair") * gcol_count + lax.axis_index("gcol")) * cond_bands
+    own_energy = lax.dynamic_slice_in_dim(cond_energy, first_band, cond_bands, 0)
+    weight = val_occupation.astype(jnp.float32)[None, :] / (
+        4.0 * (own_energy[:, None] - val_energy[None, :])
+    )
+    factor = (jnp.sqrt(weight) * (1.0 / N**1.5)).reshape(local_pairs)
+    part = pair_transform(valence, conduction, factor, gvectors)
+    prefactor = -1.0 / math.sqrt(pair_count * gcol_count * local_pairs)
+    cols, rows = exchange(part, pair_count)
+    all_pairs = pair_count * gcol_count * local_pairs
+    cols = cols.reshape(all_pairs, -1)
+    rows = rows.reshape(all_pairs, -1)
+    height = rows.shape[1] // gcol_count
+    rows = lax.dynamic_slice_in_dim(rows, lax.axis_index("gcol") * height, height, 1)
+    return pair_product(rows, cols) * prefactor
+
+
 def solution(mesh):
+    sizes = dict(mesh.shape)
+    fast = sizes["pair"] == sizes["grow"] and sizes["gcol"] == 2 and N // sizes["grow"] % 8 == 0
     return jax.shard_map(
-        body,
+        fast_body if fast else body,
         mesh=mesh,
         in_specs=(P(None, "grow", None), P(("pair", "gcol"), "grow", None), P(), P(), P(), P()),
         out_specs=P(("pair", "gcol"), "grow"),

time: 245 us -> 72.9 us (0.30)
  local copies, waits for them, and re-layouts: 94.1 us -> 1.45 us
  waiting for transfers between devices: 61.9 us -> 0 us
  Pallas kernels: 0 us -> 61.1 us
  blocking collectives: 23.9 us -> 0 us
  matrix products: 29.4 us -> 5.93 us
  between operations: 13.6 us -> 0.02 us
  other arithmetic: 15.5 us -> 3.98 us
  starting transfers between devices: 3.91 us -> 0 us
    pallas_call x0 -> x2, Pallas kernels: none -> 61.1 us  [the longest x1 36.5 us: exchange(): pl.pallas_call(exchange_kernel, out_shape=(gathered, gathered), in_specs=...]
    reshape x4 -> x0, local copies, waits for them, and re-layouts: 46.5 us -> none  [the longest x2 28.1 us: body(): second = second.reshape(local_pairs, planes, 2, extent * extent)]
    unnamed x3 -> x0, waiting for transfers between devices: 40.5 us -> none
    mul x2 -> x1, local copies, waits for them, and re-layouts: 27.4 us -> 0.08 us  [fast_body(): factor = (jnp.sqrt(weight) * (1.0 / N ** 1.5)).reshape(local_pairs)]
    dot_general x3 -> x0, matrix products: 24.2 us -> none  [the longest x1 16.8 us: body(): jnp.dot(density.reshape(-1, N), z_table, preferred_element_type=jnp.float32)]
    all_gather x2 -> x0, blocking collectives: 23.9 us -> none  [the longest x1 12.8 us: body(): full_rows = lax.all_gather(weighted, 'grow', axis=1, tiled=True)]
    reduce_scatter x1 -> x0, waiting for transfers between devices: 21.4 us -> none  [body(): lax.psum_scatter((partial_value * prefactor).astype(jnp.bfloat16), 'gcol'...]
    gather x2 -> x0, local copies, waits for them, and re-layouts: 14.2 us -> none  [body(): jnp.take(section_three, flat_index, axis=2).reshape(local_pairs, 2 * KG)]
  transfers between devices with their start and end apart: 3 -> 0, of which waited for: 2 -> 0; matrix products, arithmetic and copies ran while one was open for 0% -> 0% of each run, Pallas kernels for 0% -> 0%
where the time goes in v1:
time: 72.9 us; the launch traced here: 72.5 us
  Pallas kernels  61.1 us (84%)
  matrix products  5.93 us (8%)
  other arithmetic  3.98 us (5%)
  local copies, waits for them, and re-layouts  1.45 us (2%)
    pallas_call x1, Pallas kernels, exchange(): pl.pallas_call(exchange_kernel, out_shape=(gathered, gathered), in_specs=...  36.5 us
    pallas_call x1, Pallas kernels, pair_transform(): call(index, grow, *[valence] * 4, *[conduction] * 4, left, right, sign, p...  24.6 us
    dot_general x1, matrix products, pair_product(): lax.dot_general(left_rows, right_rows, (((0,), (0,)), ((), ())), preferre...  5.93 us

profile of v1, /device:TPU:27, one launch (start us, length us, event | category | flops | bytes accessed | tf_op | source)
XLA Modules:
  0.0 72.5 jit_solution(144822709750646173)
XLA Ops:
  0.0 0.7 %dynamic_slice.6 = f32[2]{0:T(128)S(1)} dynamic-slice(f32[16]{0:T(128)} %param.13, s32[]{:T(128)S(6)} %select_n.46), dynamic_slice_sizes={2} | dynamic-slice | bytes 20 | tf_op jit(solution)/shard_map/dynamic_slice | solution.py:389
  0.7 0.7 convert_element_type.3
  1.4 0.7 %sqrt_multiply_fusion = f32[2,16]{1,0:T(2,128)S(1)} fusion(f32[16]{0:T(128)} %param.12, f32[16]{0:T(128)S(1)} %convert_element_type.3, f32[2]{0:T(128)S(1)} %dynamic_slice.6), kind=kLoop, calls=%fused_computation.29 | loop fusion | flops 128 | bytes 264 | tf_op jit(solution)/shard_map/mul | solution.py:393
  2.1 0.1 reshape.52
  2.2 0.6 tile.9.factor
  2.8 0.9 %compare_reduce_fusion = pred[3840]{0:T(1024)(128)(4,1)S(1)} fusion(s32[3,3840]{1,0:T(4,128)} %param.15), kind=kLoop, calls=%fused_computation.2 | loop fusion | flops 3840 | bytes 19200 | tf_op jit(solution)/shard_map/lt | solution.py:245
  3.7 1.1 %abs_reduce_fusion = (s32[3840]{0:T(1024)S(1)}, s32[3840]{0:T(1024)S(1)}, s32[3840]{0:T(1024)S(1)}) fusion(s32[3,3840]{1,0:T(4,128)} %param.15), kind=kLoop, calls=%fused_computation.27 | loop fusion | flops 3840 | bytes 92160 | tf_op jit(solution)/shard_map/abs | solution.py:246
  4.8 0.6 fusion.6.idx
  5.4 24.6 %shard_map.100.part = bf16[32,7680]{1,0:T(8,128)(2,1)} custom-call(s32[3840]{0:T(1024)} %fusion.6.idx, s32[1]{0:T(128)} %bitcast.grow, bf16[16,24,9216]{2,1,0:T(8,128)(2,1)} %v3.1, bf16[16,24,9216]{2,1,0:T(8,128)(2,1)} %v3.1, bf16[16,24,9216]{2,1,0:T(8,128)(2,1)} %v3.1, bf16[16,24,9216]{2,1,0:T(8,128)(2,1)} %v3.1, bf16[2,24,9216]{2,1,0:T(8,128)(2,1)} %c3.1, ...), custom_call_target="tpu_custom_call" | custom-call | tf_op jit(solution)/shard_map/pallas_call | solution.py:291
  30.0 36.5 %shard_map.101 = (bf16[8,32,1920]{2,1,0:T(8,128)(2,1)}, bf16[8,32,1920]{2,1,0:T(8,128)(2,1)}) custom-call(bf16[32,7680]{1,0:T(8,128)(2,1)} %shard_map.100.part), custom_call_target="tpu_custom_call" | custom-call | tf_op jit(solution)/shard_map/pallas_call | solution.py:368
  66.6 5.9 %convolution_multiply_fusion = f32[960,1920]{1,0:T(8,128)} fusion(bf16[256,1920]{1,0:T(8,128)(2,1)} %bitcast.4, bf16[256,1920]{1,0:T(8,128)(2,1)} %bitcast.5, s32[]{:T(128)S(6)} %select_n.47), kind=kOutput, calls=%fused_computation | convolution fusion | flops 945561600 | bytes 8880132 | tf_op jit(solution)/shard_map/dot_general | solution.py:43
  (1 shorter events, 0.0 us)

commit v2 on v0

--- a/solution.py
+++ b/solution.py
@@ -2,7 +2,10 @@
 
 import jax
 import jax.numpy as jnp
+import numpy as np
 from jax import lax
+from jax.experimental import pallas as pl
+from jax.experimental.pallas import tpu as pltpu
 from jax.sharding import PartitionSpec as P
 
 N = 96
@@ -83,9 +86,369 @@
     ).astype(jnp.float32)
 
 
+EXT = 2 * RAD + 1
+QUARTER = N * N // 4
+STEP = 8 * N
+CLASSES = ((0, 4, 8, 12), (2, 6, 10), (1, 3, 5, 7, 9, 11))
+WIDTHS = (128, 128, 256)
+ROWS = (104, 80, 152)
+STARTS = (0, 104, 184)
+NR = 336
+
+
+def half_plane_tables():
+    total = 2 * sum(WIDTHS)
+    left = np.zeros((2, N // 4, total), np.float32)
+    right = np.zeros((2, N, total), np.float32)
+    sign = np.zeros((1, WIDTHS[2]), np.float32)
+    y = np.arange(N // 4)[:, None]
+    z = np.arange(N)[:, None]
+    k = np.arange(-RAD, RAD + 1)
+    base = 0
+    for freqs, width in zip(CLASSES, WIDTHS):
+        jj = np.repeat(np.array(freqs), EXT)[None]
+        kk = np.tile(k, len(freqs))[None]
+        count = jj.shape[1]
+        ay = 2 * np.pi * ((jj * y) % N) / N
+        az = 2 * np.pi * ((kk * z) % N) / N
+        for part in range(2):
+            cols = slice(base + part * width, base + part * width + count)
+            left[0, :, cols] = np.sin(ay) if part else np.cos(ay)
+            left[1, :, cols] = np.cos(ay) if part else -np.sin(ay)
+            right[0, :, cols] = np.cos(az)
+            right[1, :, cols] = np.sin(az)
+        base += 2 * width
+    jj = np.repeat(np.array(CLASSES[2]), EXT)
+    sign[0, : jj.size] = np.where(jj % 4 == 1, 1.0, -1.0)
+    return left, right, sign
+
+
+def plane_table(pairs):
+    x = np.arange(N)[:, None]
+    a = np.arange(1, RAD + 1)[None]
+    ang = 2 * np.pi * ((a * x) % N) / N
+    c, s = np.cos(ang), np.sin(ang)
+    tab = np.stack([np.stack([c, -s, c, -s], -1), np.stack([-s, -c, s, c], -1)])
+    return np.repeat(tab.reshape(2, N, RAD * 4), pairs, axis=2).astype(np.float32)
+
+
+def chi_kernel(
+    idx, occ, val_e, cond_e, v0, v1, v2, v3, c0, c1, c2, c3, left, right, sign, xtab,
+    cols_out, rows_out,
+    ee, eo, oo, tabs, acc_ee, acc_eo, acc_o, xmat, sec, got, part, inbox, blocks, cols, rows,
+    sends, recvs, outs,
+):
+    band, step = pl.program_id(0), pl.program_id(1)
+    bands, steps = part.shape[0], tabs.shape[0]
+    nv, planes, _ = v0.shape
+    height = nv * planes
+    lanes = 128
+    per_tile = lanes // (4 * nv)
+    f32, bf16 = jnp.float32, jnp.bfloat16
+    _, count, _, width = blocks.shape
+    n = count - 1
+    p, g, c = lax.axis_index("pair"), lax.axis_index("grow"), lax.axis_index("gcol")
+    me = p * 2 + c
+    turn = lambda at, k: lax.rem(at + k, count)
+    block = lambda at: pl.ds(pl.multiple_of(at * width, 128), width)
+
+    def copy_of(h, src, dst, sem, to):
+        return pltpu.make_async_remote_copy(
+            src_ref=src, dst_ref=dst, send_sem=sends.at[h, sem], recv_sem=recvs.at[h, sem],
+            device_id=to, device_id_type=pl.DeviceIdType.MESH,
+        )
+
+    def first(h, k):
+        return copy_of(
+            h, part.at[h, :, block(turn(g, k))], inbox.at[h, k - 1], k - 1, (p, turn(g, k), c)
+        )
+
+    def along(h, k):
+        return copy_of(h, blocks.at[h, g], blocks.at[h, g], n + k - 1, (p, turn(g, k), c))
+
+    def flat(h, k):
+        return copy_of(h, cols.at[me, h], cols.at[me, h], 2 * n + k - 1, (turn(p, k), g, c))
+
+    def across(h, k):
+        return copy_of(
+            h, blocks.at[h, turn(p, k)], rows.at[me, h], 3 * n + k - 1, (turn(p, k), g, c)
+        )
+
+    def over(h, k, ref, base):
+        slot = turn(p, count - k) * 2 + c
+        return copy_of(h, ref.at[slot, h], ref.at[slot, h], base + k, (p, g, 1 - c))
+
+    def stage_send(h):
+        for k in range(1, count):
+            first(h, k).start()
+
+    def stage_sum(h):
+        total = part[h, :, block(g)].astype(f32)
+        for k in range(1, count):
+            first(h, k).wait_recv()
+            total += inbox[h, k - 1].astype(f32)
+        mine = total.astype(bf16)
+        blocks[h, g] = mine
+        cols[me, h] = mine
+        for k in range(1, count):
+            along(h, k).start()
+        for k in range(1, count):
+            flat(h, k).start()
+        over(h, 0, cols, 4 * n).start()
+
+    def stage_across(h):
+        for k in range(1, count):
+            along(h, k).wait_recv()
+        for k in range(1, count):
+            across(h, k).start()
+        rows[me, h] = blocks[h, p]
+        over(h, 0, rows, 5 * n + 1).start()
+        for k in range(1, count):
+            flat(h, k).wait_recv()
+            over(h, k, cols, 4 * n).start()
+
+    def stage_rows(h):
+        for k in range(1, count):
+            across(h, k).wait_recv()
+            over(h, k, rows, 5 * n + 1).start()
+
+    @pl.when((band == 0) & (step == 0))
+    def _():
+        barrier = pltpu.get_barrier_semaphore()
+        for k in range(1, count):
+            pl.semaphore_signal(barrier, inc=1, device_id=(p, turn(g, k), c))
+            pl.semaphore_signal(barrier, inc=1, device_id=(turn(p, k), g, c))
+        pl.semaphore_signal(barrier, inc=1, device_id=(p, g, 1 - c))
+        pl.semaphore_wait(barrier, 2 * count - 1)
+
+    @pl.when(band == 0)
+    def _():
+        for y in range(STEP // N):
+            yy = step * (STEP // N) + y
+            l1 = left[0, pl.ds(yy, 1), :]
+            l2 = left[1, pl.ds(yy, 1), :]
+            tabs[step, y * N : (y + 1) * N, :] = (l1 * right[0] + l2 * right[1]).astype(bf16)
+
+    @pl.when(step == 0)
+    def _():
+        acc_ee[...] = jnp.zeros_like(acc_ee)
+        acc_eo[...] = jnp.zeros_like(acc_eo)
+        acc_o[...] = jnp.zeros_like(acc_o)
+
+    def products(v, carry):
+        d0, d1, d2, d3 = [
+            (a[pl.ds(2 * v, 2)].astype(f32) * b[band].astype(f32)[None]).reshape(2 * planes, STEP)
+            for a, b in ((v0, c0), (v1, c1), (v2, c2), (v3, c3))
+        ]
+        e0, e1 = d0 + d2, d1 + d3
+        at = pl.multiple_of(v * 2 * planes, 16)
+        where = pl.ds(at, 2 * planes)
+        ee[where, :] = (e0 + e1).astype(bf16)
+        eo[where, :] = (e0 - e1).astype(bf16)
+        oo[where, :] = (d0 - d2).astype(bf16)
+        oo[pl.ds(pl.multiple_of(height + at, 16), 2 * planes), :] = (d1 - d3).astype(bf16)
+        return carry
+
+    lax.fori_loop(0, nv // 2, products, 0)
+    acc_ee[...] += jnp.dot(ee[...], tabs[step, :, 0:256], preferred_element_type=f32)
+    acc_eo[...] += jnp.dot(eo[...], tabs[step, :, 256:512], preferred_element_type=f32)
+
+    def multiply(i, carry):
+        at = pl.ds(pl.multiple_of(i * height, 16), height)
+        acc_o[at, :] += jnp.dot(oo[at, :], tabs[step, :, 512:1024], preferred_element_type=f32)
+        return carry
+
+    lax.fori_loop(0, 2, multiply, 0)
+
+    for h in range(1, bands):
+        @pl.when((band == h) & (step == steps - 2))
+        def _():
+            stage_sum(h - 1)
+
+        @pl.when((band == h) & (step == steps - 1))
+        def _():
+            stage_across(h - 1)
+
+    @pl.when((band == 0) & (step == 0))
+    def _():
+        own = lax.broadcasted_iota(jnp.int32, (1, RAD * 4 * nv), 1) % nv
+
+        weights = [xtab[h, pl.ds(pl.multiple_of(g * planes, 8), planes), :] for h in range(2)]
+
+        def place(v, carry):
+            for h in range(2):
+                two = [jnp.where(own == 2 * v + u, weights[h], 0.0) for u in range(2)]
+                at = pl.multiple_of(h * height + v * 2 * planes, 16)
+                xmat[pl.ds(at, 2 * planes), :] = jnp.concatenate(two, 0).astype(bf16)
+            return carry
+
+        lax.fori_loop(0, nv // 2, place, 0)
+
+    @pl.when(step == steps - 1)
+    def _():
+        lane = lax.broadcasted_iota(jnp.int32, (1, lanes), 1) % nv
+        occupied = jnp.zeros((1, lanes), jnp.int32)
+        energy = jnp.zeros((1, lanes), f32)
+        for v in range(nv):
+            occupied = jnp.where(lane == v, occ[v], occupied)
+            energy = jnp.where(lane == v, val_e[v], energy)
+        gap = cond_e[me * bands + band] - energy
+        factor = jnp.sqrt(occupied.astype(f32) / (4.0 * gap)) * (1.0 / N**1.5)
+        w = WIDTHS[2]
+        top, low = acc_o[0:height, :], acc_o[height : 2 * height, :]
+        odd_p = top[:, 0:w] - sign[...] * low[:, w:]
+        odd_q = top[:, w:] + sign[...] * low[:, 0:w]
+        groups = (
+            (acc_ee[:, 0:128], acc_ee[:, 128:256]),
+            (acc_eo[:, 0:128], acc_eo[:, 128:256]),
+            (odd_p, odd_q),
+        )
+        for (p_part, q_part), size, start in zip(groups, ROWS, STARTS):
+            p_rows = p_part.T[0:size].astype(bf16)
+            q_rows = q_part.T[0:size].astype(bf16)
+            summed = jnp.dot(p_rows, xmat[0:height, :], preferred_element_type=f32)
+            summed += jnp.dot(q_rows, xmat[height : 2 * height, :], preferred_element_type=f32)
+            for t in range(RAD // per_tile):
+                piece = summed[:, t * lanes : (t + 1) * lanes] * factor
+                for u in range(2 * per_tile):
+                    a = t * per_tile + u // 2
+                    at = ((u % 2) * RAD + a) * NR + start
+                    turned = pltpu.roll(piece, lanes - 2 * nv * u, 1) if u else piece
+                    sec[at : at + size, :] = turned
+
+        def pick(i, carry):
+            for u in range(16):
+                got[pl.ds(i * 16 + u, 1), :] = sec[pl.ds(idx[i * 16 + u], 1), :]
+            return carry
+
+        lax.fori_loop(0, KG // 16, pick, 0)
+        for i in range(KG // 384):
+            turned = got[i * 384 : (i + 1) * 384, :].T.astype(bf16)
+            part[band, :, i * 384 : (i + 1) * 384] = turned[0:nv]
+            part[band, :, KG + i * 384 : KG + (i + 1) * 384] = turned[nv : 2 * nv]
+
+    for h in range(bands):
+        @pl.when((band == h) & (step == steps - 1))
+        def _():
+            stage_send(h)
+            if h:
+                stage_rows(h - 1)
+            if h == bands - 1:
+                stage_sum(h)
+                stage_across(h)
+                stage_rows(h)
+                for q in range(bands):
+                    for k in range(count):
+                        over(q, k, cols, 4 * n).wait_recv()
+                first_out = pltpu.make_async_copy(cols, cols_out, outs.at[0])
+                first_out.start()
+                for q in range(bands):
+                    for k in range(count):
+                        over(q, k, rows, 5 * n + 1).wait_recv()
+                second_out = pltpu.make_async_copy(rows, rows_out, outs.at[1])
+                second_out.start()
+                for q in range(bands):
+                    for k in range(1, count):
+                        first(q, k).wait_send()
+                        along(q, k).wait_send()
+                        flat(q, k).wait_send()
+                        across(q, k).wait_send()
+                    for k in range(count):
+                        over(q, k, cols, 4 * n).wait_send()
+                        over(q, k, rows, 5 * n + 1).wait_send()
+                first_out.wait()
+                second_out.wait()
+
+
+def row_index(gvectors):
+    a, b, d = gvectors[0], gvectors[1], gvectors[2]
+    flip = b < 0
+    j = jnp.abs(b)
+    k = jnp.where(flip, -d, d) + RAD
+    row = jnp.where(
+        j % 2 == 1,
+        STARTS[2] + (j // 2) * EXT,
+        jnp.where(j % 4 == 2, STARTS[1], STARTS[0]) + (j // 4) * EXT,
+    )
+    return (jnp.where(flip, RAD, 0) + a - 1) * NR + row + k
+
+
+def fast_body(valence, conduction, val_energy, cond_energy, val_occupation, gvectors):
+    nv, planes, _ = valence.shape
+    bands = conduction.shape[0]
+    count = lax.axis_size("pair")
+    gcol_count = lax.axis_size("gcol")
+    height = nv * planes
+    steps = QUARTER // STEP
+    width = 2 * KG // count
+    slots = count * gcol_count
+    bf16, f32 = jnp.bfloat16, jnp.float32
+    left, right, sign = half_plane_tables()
+    whole = lambda shape: pl.BlockSpec(shape, lambda b, i, idx: (0,) * len(shape))
+    piece = lambda size, q: pl.BlockSpec(
+        (size, planes, STEP), lambda b, i, idx, q=q: (0, 0, q * steps + i)
+    )
+    smem = pl.BlockSpec(memory_space=pltpu.SMEM)
+    gathered = jax.ShapeDtypeStruct((slots, bands, nv, width), bf16)
+    sems = 6 * (count - 1) + 2
+    cols, rows = pl.pallas_call(
+        chi_kernel,
+        out_shape=(gathered, gathered),
+        grid_spec=pltpu.PrefetchScalarGridSpec(
+            num_scalar_prefetch=1,
+            grid=(bands, steps),
+            in_specs=[smem] * 3
+            + [piece(nv, q) for q in range(4)]
+            + [piece(bands, q) for q in range(4)]
+            + [
+                whole(left.shape),
+                whole(right.shape),
+                whole(sign.shape),
+                whole((2, N, RAD * 4 * nv)),
+            ],
+            out_specs=(pl.BlockSpec(memory_space=pl.ANY), pl.BlockSpec(memory_space=pl.ANY)),
+            scratch_shapes=[
+                pltpu.VMEM((height, STEP), bf16),
+                pltpu.VMEM((height, STEP), bf16),
+                pltpu.VMEM((2 * height, STEP), bf16),
+                pltpu.VMEM((steps, STEP, 2 * sum(WIDTHS)), bf16),
+                pltpu.VMEM((height, 2 * WIDTHS[0]), f32),
+                pltpu.VMEM((height, 2 * WIDTHS[1]), f32),
+                pltpu.VMEM((2 * height, 2 * WIDTHS[2]), f32),
+                pltpu.VMEM((2 * height, RAD * 4 * nv), bf16),
+                pltpu.VMEM((2 * RAD * NR, 128), f32),
+                pltpu.VMEM((KG, 128), f32),
+                pltpu.VMEM((bands, nv, 2 * KG), bf16),
+                pltpu.VMEM((bands, count - 1, nv, width), bf16),
+                pltpu.VMEM((bands, count, nv, width), bf16),
+                pltpu.VMEM((slots, bands, nv, width), bf16),
+                pltpu.VMEM((slots, bands, nv, width), bf16),
+                pltpu.SemaphoreType.DMA((bands, sems)),
+                pltpu.SemaphoreType.DMA((bands, sems)),
+                pltpu.SemaphoreType.DMA((2,)),
+            ],
+        ),
+        compiler_params=pltpu.CompilerParams(
+            vmem_limit_bytes=60 * 1024 * 1024, collective_id=0, has_side_effects=True
+        ),
+    )(
+        row_index(gvectors), val_occupation, val_energy, cond_energy,
+        *([valence] * 4), *([conduction] * 4), left, right, sign, plane_table(nv),
+    )
+    all_pairs = slots * bands * nv
+    prefactor = -1.0 / math.sqrt(all_pairs)
+    cols = cols.reshape(all_pairs, width)
+    rows = rows.reshape(all_pairs, width)
+    share = width // gcol_count
+    rows = lax.dynamic_slice_in_dim(rows, lax.axis_index("gcol") * share, share, 1)
+    return pair_product(rows, cols) * prefactor
+
+
 def solution(mesh):
+    sizes = dict(mesh.shape)
+    fast = sizes["pair"] == sizes["grow"] and sizes["gcol"] == 2 and N // sizes["grow"] % 8 == 0
     return jax.shard_map(
-        body,
+        fast_body if fast else body,
         mesh=mesh,
         in_specs=(P(None, "grow", None), P(("pair", "gcol"), "grow", None), P(), P(), P(), P()),
         out_specs=P(("pair", "gcol"), "grow"),

time: 245 us -> 69 us (0.28)
  the two profiles are of different devices: /device:TPU:27 before, /device:TPU:1 now
where the time goes in v2:
time: 69 us; the launch traced here: 68.7 us
  Pallas kernels  60.2 us (87%)
  matrix products  5.93 us (9%)
  other arithmetic  2.6 us (4%)
    pallas_call x1, Pallas kernels, fast_body(): pl.pallas_call(chi_kernel, out_shape=(gathered, gathered), grid_spec=pltp...  60.2 us
    dot_general x1, matrix products, pair_product(): lax.dot_general(left_rows, right_rows, (((0,), (0,)), ((), ())), preferre...  5.93 us

profile of v2, /device:TPU:1, one launch (start us, length us, event | category | flops | bytes accessed | tf_op | source)
XLA Modules:
  0.0 68.7 jit_solution(14963671369484342601)
XLA Ops:
  0.0 0.9 %compare_reduce_fusion = pred[3840]{0:T(1024)(128)(4,1)S(1)} fusion(s32[3,3840]{1,0:T(4,128)} %param.15), kind=kLoop, calls=%fused_computation.2 | loop fusion | flops 3840 | bytes 19200 | tf_op jit(solution)/shard_map/lt | solution.py:365
  0.9 1.1 %abs_reduce_fusion = (s32[3840]{0:T(1024)S(1)}, s32[3840]{0:T(1024)S(1)}, s32[3840]{0:T(1024)S(1)}) fusion(s32[3,3840]{1,0:T(4,128)} %param.15), kind=kLoop, calls=%fused_computation.27 | loop fusion | flops 3840 | bytes 92160 | tf_op jit(solution)/shard_map/abs | solution.py:366
  2.0 0.6 fusion.6.idx
  2.6 60.2 %shard_map.100 = (bf16[8,2,16,1920]{3,2,1,0:T(8,128)(2,1)}, bf16[8,2,16,1920]{3,2,1,0:T(8,128)(2,1)}) custom-call(s32[3840]{0:T(1024)} %fusion.6.idx, s32[16]{0:T(128)} %occ.1, f32[16]{0:T(128)} %val_e.1, f32[16]{0:T(128)} %cond_e.1, bf16[16,24,9216]{2,1,0:T(8,128)(2,1)} %v3.1, bf16[16,24,9216]{2,1,0:T(8,128)(2,1)} %v3.1, bf16[16,24,9216]{2,1,0:T(8,128)(2,1)} %v3.1, ...), custom_call_target="tpu_custom_call" | custom-call | tf_op jit(solution)/shard_map/pallas_call | solution.py:394
  62.8 5.9 %convolution_multiply_fusion = f32[960,1920]{1,0:T(8,128)} fusion(bf16[256,1920]{1,0:T(8,128)(2,1)} %bitcast.3, bf16[256,1920]{1,0:T(8,128)(2,1)} %bitcast.4, s32[]{:T(128)S(6)} %select_n.43), kind=kOutput, calls=%fused_computation | convolution fusion | flops 945561600 | bytes 8880132 | tf_op jit(solution)/shard_map/dot_general | solution.py:41

commit v3 on v2

--- a/solution.py
+++ b/solution.py
@@ -1,3 +1,4 @@
+import functools
 import math
 
 import jax
@@ -132,11 +133,23 @@
     return np.repeat(tab.reshape(2, N, RAD * 4), pairs, axis=2).astype(np.float32)
 
 
+def row_index(a, b, d):
+    flip = b < 0
+    j = jnp.abs(b)
+    k = jnp.where(flip, -d, d) + RAD
+    row = jnp.where(
+        (j & 1) == 1,
+        STARTS[2] + (j >> 1) * EXT,
+        jnp.where((j & 3) == 2, STARTS[1], STARTS[0]) + (j >> 2) * EXT,
+    )
+    return jnp.maximum((jnp.where(flip, RAD, 0) + a - 1) * NR + row + k, 0)
+
+
 def chi_kernel(
-    idx, occ, val_e, cond_e, v0, v1, v2, v3, c0, c1, c2, c3, left, right, sign, xtab,
+    occ, val_e, cond_e, gvec, v0, v1, v2, v3, c0, c1, c2, c3, left, right, sign, xtab,
     cols_out, rows_out,
     ee, eo, oo, tabs, acc_ee, acc_eo, acc_o, xmat, sec, got, part, inbox, blocks, cols, rows,
-    sends, recvs, outs,
+    index, idx, sends, recvs, outs,
 ):
     band, step = pl.program_id(0), pl.program_id(1)
     bands, steps = part.shape[0], tabs.shape[0]
@@ -178,9 +191,17 @@
         slot = turn(p, count - k) * 2 + c
         return copy_of(h, ref.at[slot, h], ref.at[slot, h], base + k, (p, g, 1 - c))
 
-    def stage_send(h):
-        for k in range(1, count):
-            first(h, k).start()
+    def pass_on(h, b):
+        @pl.when(b != p)
+        def _():
+            copy_of(
+                h, blocks.at[h, b], rows.at[me, h], 3 * n + turn(b, count - p) - 1, (b, g, c)
+            ).start()
+
+        @pl.when(b == p)
+        def _():
+            rows[me, h] = blocks[h, p]
+            over(h, 0, rows, 5 * n + 1).start()
 
     def stage_sum(h):
         total = part[h, :, block(g)].astype(f32)
@@ -195,17 +216,14 @@
         for k in range(1, count):
             flat(h, k).start()
         over(h, 0, cols, 4 * n).start()
+        pass_on(h, g)
 
     def stage_across(h):
-        for k in range(1, count):
-            along(h, k).wait_recv()
-        for k in range(1, count):
-            across(h, k).start()
-        rows[me, h] = blocks[h, p]
-        over(h, 0, rows, 5 * n + 1).start()
         for k in range(1, count):
             flat(h, k).wait_recv()
             over(h, k, cols, 4 * n).start()
+            along(h, k).wait_recv()
+            pass_on(h, turn(g, count - k))
 
     def stage_rows(h):
         for k in range(1, count):
@@ -214,12 +232,13 @@
 
     @pl.when((band == 0) & (step == 0))
     def _():
+        index[...] = row_index(gvec[0:1, :], gvec[1:2, :], gvec[2:3, :])
+        pltpu.make_async_copy(index, idx, outs.at[0]).start()
         barrier = pltpu.get_barrier_semaphore()
         for k in range(1, count):
             pl.semaphore_signal(barrier, inc=1, device_id=(p, turn(g, k), c))
             pl.semaphore_signal(barrier, inc=1, device_id=(turn(p, k), g, c))
         pl.semaphore_signal(barrier, inc=1, device_id=(p, g, 1 - c))
-        pl.semaphore_wait(barrier, 2 * count - 1)
 
     @pl.when(band == 0)
     def _():
@@ -259,6 +278,11 @@
         return carry
 
     lax.fori_loop(0, 2, multiply, 0)
+
+    @pl.when((band == 0) & (step == steps - 1))
+    def _():
+        pltpu.make_async_copy(index, idx, outs.at[0]).wait()
+        pl.semaphore_wait(pltpu.get_barrier_semaphore(), 2 * count - 1)
 
     for h in range(1, bands):
         @pl.when((band == h) & (step == steps - 2))
@@ -318,19 +342,24 @@
 
         def pick(i, carry):
             for u in range(16):
-                got[pl.ds(i * 16 + u, 1), :] = sec[pl.ds(idx[i * 16 + u], 1), :]
+                got[pl.ds(i * 16 + u, 1), :] = sec[pl.ds(idx[0, i * 16 + u], 1), :]
             return carry
 
-        lax.fori_loop(0, KG // 16, pick, 0)
-        for i in range(KG // 384):
-            turned = got[i * 384 : (i + 1) * 384, :].T.astype(bf16)
-            part[band, :, i * 384 : (i + 1) * 384] = turned[0:nv]
-            part[band, :, KG + i * 384 : KG + (i + 1) * 384] = turned[nv : 2 * nv]
+        halves = KG // width
+        for q in range(halves):
+            lax.fori_loop(q * width // 16, (q + 1) * width // 16, pick, 0)
+            for i in range(q * width // 384, (q + 1) * width // 384):
+                turned = got[i * 384 : (i + 1) * 384, :].T.astype(bf16)
+                part[band, :, i * 384 : (i + 1) * 384] = turned[0:nv]
+                part[band, :, KG + i * 384 : KG + (i + 1) * 384] = turned[nv : 2 * nv]
+            for k in range(1, count):
+                @pl.when(lax.rem(turn(g, k), halves) == q)
+                def _():
+                    first(band, k).start()
 
     for h in range(bands):
         @pl.when((band == h) & (step == steps - 1))
         def _():
-            stage_send(h)
             if h:
                 stage_rows(h - 1)
             if h == bands - 1:
@@ -360,17 +389,36 @@
                 second_out.wait()
 
 
-def row_index(gvectors):
-    a, b, d = gvectors[0], gvectors[1], gvectors[2]
-    flip = b < 0
-    j = jnp.abs(b)
-    k = jnp.where(flip, -d, d) + RAD
-    row = jnp.where(
-        j % 2 == 1,
-        STARTS[2] + (j // 2) * EXT,
-        jnp.where(j % 4 == 2, STARTS[1], STARTS[0]) + (j // 4) * EXT,
-    )
-    return (jnp.where(flip, RAD, 0) + a - 1) * NR + row + k
+def product_kernel(prefactor, rows, cols, out, turned):
+    share, tile = out.shape
+    c = lax.axis_index("gcol")
+    low = share // 128 * 128
+    shift = share - low
+
+    @pl.when(pl.program_id(0) == 0)
+    def _():
+        span = turned.shape[0]
+        turned[...] = rows[:, pl.ds(pl.multiple_of(c * low, 128), span)].T
+
+    left = turned[pl.ds(pl.multiple_of(c * shift, 16), share), :]
+    out[...] = jnp.dot(left, cols[...], preferred_element_type=jnp.float32) * prefactor
+
+
+def product(rows, cols, share, prefactor):
+    depth, width = rows.shape
+    low = share // 128 * 128
+    tile = 384
+    return pl.pallas_call(
+        functools.partial(product_kernel, prefactor),
+        out_shape=jax.ShapeDtypeStruct((share, width), jnp.float32),
+        grid=(width // tile,),
+        in_specs=[
+            pl.BlockSpec((depth, width), lambda i: (0, 0)),
+            pl.BlockSpec((depth, tile), lambda i: (0, i)),
+        ],
+        out_specs=pl.BlockSpec((share, tile), lambda i: (0, i)),
+        scratch_shapes=[pltpu.VMEM((width - low, depth), jnp.bfloat16)],
+    )(rows, cols)
 
 
 def fast_body(valence, conduction, val_energy, cond_energy, val_occupation, gvectors):
@@ -384,9 +432,9 @@
     slots = count * gcol_count
     bf16, f32 = jnp.bfloat16, jnp.float32
     left, right, sign = half_plane_tables()
-    whole = lambda shape: pl.BlockSpec(shape, lambda b, i, idx: (0,) * len(shape))
+    whole = lambda shape: pl.BlockSpec(shape, lambda b, i: (0,) * len(shape))
     piece = lambda size, q: pl.BlockSpec(
-        (size, planes, STEP), lambda b, i, idx, q=q: (0, 0, q * steps + i)
+        (size, planes, STEP), lambda b, i, q=q: (0, 0, q * steps + i)
     )
     smem = pl.BlockSpec(memory_space=pltpu.SMEM)
     gathered = jax.ShapeDtypeStruct((slots, bands, nv, width), bf16)
@@ -395,9 +443,10 @@
         chi_kernel,
         out_shape=(gathered, gathered),
         grid_spec=pltpu.PrefetchScalarGridSpec(
-            num_scalar_prefetch=1,
+            num_scalar_prefetch=0,
             grid=(bands, steps),
             in_specs=[smem] * 3
+            + [whole((3, KG))]
             + [piece(nv, q) for q in range(4)]
             + [piece(bands, q) for q in range(4)]
             + [
@@ -423,6 +472,8 @@
                 pltpu.VMEM((bands, count, nv, width), bf16),
                 pltpu.VMEM((slots, bands, nv, width), bf16),
                 pltpu.VMEM((slots, bands, nv, width), bf16),
+                pltpu.VMEM((1, KG), jnp.int32),
+                pltpu.SMEM((1, KG), jnp.int32),
                 pltpu.SemaphoreType.DMA((bands, sems)),
                 pltpu.SemaphoreType.DMA((bands, sems)),
                 pltpu.SemaphoreType.DMA((2,)),
@@ -432,7 +483,7 @@
             vmem_limit_bytes=60 * 1024 * 1024, collective_id=0, has_side_effects=True
         ),
     )(
-        row_index(gvectors), val_occupation, val_energy, cond_energy,
+        val_occupation, val_energy, cond_energy, gvectors,
         *([valence] * 4), *([conduction] * 4), left, right, sign, plane_table(nv),
     )
     all_pairs = slots * bands * nv
@@ -440,8 +491,7 @@
     cols = cols.reshape(all_pairs, width)
     rows = rows.reshape(all_pairs, width)
     share = width // gcol_count
-    rows = lax.dynamic_slice_in_dim(rows, lax.axis_index("gcol") * share, share, 1)
-    return pair_product(rows, cols) * prefactor
+    return product(rows, cols, share, prefactor)
 
 
 def solution(mesh):

time: 69 us -> 59.4 us (0.86)
  the two profiles are of different devices: /device:TPU:1 before, /device:TPU:27 now
where the time goes in v3:
time: 59.4 us; the launch traced here: 58.7 us
  Pallas kernels  58.7 us (99%)
    pallas_call x1, Pallas kernels, fast_body(): pl.pallas_call(chi_kernel, out_shape=(gathered, gathered), grid_spec=pltp...  52.5 us
    pallas_call x1, Pallas kernels, product(): pl.pallas_call(functools.partial(product_kernel, prefactor), out_shape=ja...  6.26 us

profile of v3, /device:TPU:27, one launch (start us, length us, event | category | flops | bytes accessed | tf_op | source)
XLA Modules:
  0.0 58.7 jit_solution(14785838684674821772)
XLA Ops:
  0.0 52.5 %shard_map.100 = (bf16[8,2,16,1920]{3,2,1,0:T(8,128)(2,1)}, bf16[8,2,16,1920]{3,2,1,0:T(8,128)(2,1)}) custom-call(s32[16]{0:T(128)} %occ.1, f32[16]{0:T(128)} %val_e.1, f32[16]{0:T(128)} %cond_e.1, s32[3,3840]{1,0:T(4,128)} %gvec.1, bf16[16,24,9216]{2,1,0:T(8,128)(2,1)} %v3.1, bf16[16,24,9216]{2,1,0:T(8,128)(2,1)} %v3.1, bf16[16,24,9216]{2,1,0:T(8,128)(2,1)} %v3.1, ...), custom_call_target="tpu_custom_call" | custom-call | tf_op jit(solution)/shard_map/pallas_call | solution.py:442
  52.5 6.3 %shard_map.101 = f32[960,1920]{1,0:T(8,128)} custom-call(bf16[256,1920]{1,0:T(8,128)(2,1)} %bitcast.3, bf16[256,1920]{1,0:T(8,128)(2,1)} %bitcast.2), custom_call_target="tpu_custom_call" | custom-call | tf_op jit(solution)/shard_map/pallas_call | solution.py:411
